TPU v7x, 32 devices: a whole 2x2x4 slice. The times are simulated.
32 devices in a mesh: row: 4 (over y, core), col: 8 (over z, x).
Axes of the slice: x: 2, y: 2, z: 4, core: 2. Of those that a mesh axis runs over, the one named last changes fastest.
Arguments:
- values: bfloat16 [8192, 128], P('row'), may hold values from -30 to 30
- points0: bfloat16 [2, 8192], P(None, 'row'), may hold values from 0 to 1
- points1: bfloat16 [2, 2048], P(None, 'row'), may hold values from 0 to 1
- points2: bfloat16 [2, 256], P(None, 'row'), may hold values from 0 to 1
- tiles_a0: int32 [4, 8, 2, 48], P('row', 'col'), may hold values from 0 to 15, as said below
- tiles_e1: int32 [4, 8, 2, 20], P('row', 'col'), may hold values from 0 to 15, as said below
- tiles_a1: int32 [4, 8, 2, 4], P('row', 'col'), may hold values from 0 to 3, as said below
- factor: bfloat16 [256, 256], P('row', 'col'), as said below
Outputs:
- fine_coef: float32 [8192, 128], P(('row', 'col'))
- mid_coef: float32 [2048, 128], P('col')
- coarse_coef: float32 [256, 128], P('row')
- norms: float32 [1], replicated
Inputs may be any that keep to these rules, and one draw needn't show every extreme that they name: `tiles_a0`: within each block the 48 listed tile pairs are distinct; tile rows are below 16 and tile columns below 8. `tiles_e1`: within each block the 20 listed tile pairs are distinct; tile rows are below 16 and tile columns below 2. `tiles_a1`: within each block the 4 listed tile pairs are distinct; tile rows are below 4 and tile columns below 2. `factor`: upper triangular; diagonal entries from 1 to 2.
All inputs are finite; a program needn't handle non-finite values.
Results may differ from a plain program's by a relative error of at most 0.0042.
Values may be sent and summed in bfloat16 or wider, within the bound.
A program may use at most 64 MiB of HBM per device.

v0:
```python
import math
import jax
import jax.numpy as jnp
from jax import lax
from jax.sharding import PartitionSpec as P

TILE = 128
support_fine = 0.35
support_mid = 0.55
support_coarse = 0.8


def spread(x, axis, root):
    mine = lax.axis_index(axis) == root
    return lax.psum(jnp.where(mine, x, jnp.zeros_like(x)), axis)


def wendland(left_pts, right_pts, support):
    left = left_pts.astype(jnp.float32)
    right = right_pts.astype(jnp.float32)
    across = left[0][..., :, None] - right[0][..., None, :]
    upward = left[1][..., :, None] - right[1][..., None, :]
    ratio_t = jnp.sqrt(across * across + upward * upward) / support
    margin = jnp.maximum(1.0 - ratio_t, 0.0)
    squared = margin * margin
    return (squared * squared * (4.0 * ratio_t + 1.0)).astype(jnp.bfloat16)


def listed_terms(row_pts, col_pts, listing, vector, support, flipped):
    row_tiles = row_pts.reshape(2, -1, TILE)
    col_tiles = col_pts.reshape(2, -1, TILE)
    listed = listing.shape[-1]
    group = math.gcd(listed, 32)
    order = listing.reshape(2, listed // group, group)
    fields = vector.shape[-1]
    inputs = vector.reshape(-1, TILE, fields)
    target = col_tiles.shape[1] if flipped else row_tiles.shape[1]
    total = jnp.zeros((target, TILE, fields), jnp.float32)

    def add_group(total, pair):
        tile_rows, tile_cols = pair
        kernel = wendland(row_tiles[:, tile_rows], col_tiles[:, tile_cols], support)
        if flipped:
            contrib = jnp.einsum(
                "gij,gir->gjr", kernel, inputs[tile_rows], preferred_element_type=jnp.float32
            )
            return (total.at[tile_cols].add(contrib), None)
        contrib = jnp.einsum(
            "gij,gjr->gir", kernel, inputs[tile_cols], preferred_element_type=jnp.float32
        )
        return (total.at[tile_rows].add(contrib), None)

    total, unused = lax.scan(add_group, total, (order[0], order[1]))
    return total.reshape(-1, fields)


def per_device(values, points0, points1, points2, tiles_a0, tiles_e1, tiles_a1, factor):
    row_count = lax.axis_size("row")
    col_count = lax.axis_size("col")
    col_id = lax.axis_index("col")
    col_per_row = col_count // row_count
    rows_fine, fields = values.shape
    rows_mid = points1.shape[1]
    share = rows_fine // col_count
    cols_fine = rows_fine // col_per_row
    cols_mid = rows_mid // col_per_row
    source = col_id // col_per_row
    part_index = col_id % col_per_row
    value_piece = lax.dynamic_slice_in_dim(values, part_index * cols_fine, cols_fine, 0)
    fine_piece = lax.dynamic_slice_in_dim(points0, part_index * cols_fine, cols_fine, 1)
    mid_piece = lax.dynamic_slice_in_dim(points1, part_index * cols_mid, cols_mid, 1)
    value_cols, fine_cols, mid_cols = (
        spread(value_piece, "row", source),
        spread(fine_piece, "row", source),
        spread(mid_piece, "row", source),
    )
    scale_a0 = (rows_fine / (col_count * tiles_a0.shape[-1] * TILE * TILE)) ** 0.5
    scale_e1 = (rows_fine / (col_count * tiles_e1.shape[-1] * TILE * TILE)) ** 0.5
    scale_a1 = (rows_mid / (col_count * tiles_a1.shape[-1] * TILE * TILE)) ** 0.5
    scale_e2 = (1.0 / (rows_mid * row_count)) ** 0.5
    fine_data = values.astype(jnp.float32)
    own_data = lax.dynamic_slice_in_dim(values, col_id * share, share, 0).astype(jnp.float32)
    product_part = listed_terms(points0, fine_cols, tiles_a0[0, 0], value_cols, support_fine, False)
    product_whole = lax.psum(product_part, "col")
    fine_residual = fine_data - 0.5 * (scale_a0 * product_whole)
    fine_square = jnp.sum(fine_residual * fine_residual)
    restrict_part = listed_terms(
        points0, mid_cols, tiles_e1[0, 0], fine_residual.astype(jnp.bfloat16), support_mid, True
    )
    restrict_sum = lax.psum(restrict_part, "row")
    mid_data = scale_e1 * restrict_sum
    mid_part = listed_terms(
        points1, mid_cols, tiles_a1[0, 0], mid_data.astype(jnp.bfloat16), support_mid, False
    )
    mid_whole = (scale_a1 * lax.psum(mid_part, "col")).astype(jnp.bfloat16)
    mid_slice = lax.dynamic_slice_in_dim(mid_whole, part_index * cols_mid, cols_mid, 0)
    mid_turned = spread(mid_slice, "row", source)
    mid_residual = mid_data - 0.5 * mid_turned.astype(jnp.float32)
    coarse_kernel = wendland(points2, mid_cols, support_coarse)
    coarse_part = jnp.dot(
        coarse_kernel, mid_residual.astype(jnp.bfloat16), preferred_element_type=jnp.float32
    )
    coarse_sum = lax.psum(coarse_part, "col")
    coarse_data = (scale_e2 * coarse_sum).astype(jnp.bfloat16)
    halfway_part = lax.dot_general(
        factor, coarse_data, (((0,), (0,)), ((), ())), preferred_element_type=jnp.float32
    )
    halfway = lax.psum(halfway_part, "row").astype(jnp.bfloat16)
    coarse_part_two = jnp.dot(factor, halfway, preferred_element_type=jnp.float32)
    coarse_coef = lax.psum(coarse_part_two, "col")
    prolong_part = lax.dot_general(
        coarse_kernel,
        coarse_coef.astype(jnp.bfloat16),
        (((0,), (0,)), ((), ())),
        preferred_element_type=jnp.float32,
    )
    mid_coef = 0.5 * mid_data + scale_e2 * lax.psum(prolong_part, "row")
    fine_part = listed_terms(
        points0, mid_cols, tiles_e1[0, 0], mid_coef.astype(jnp.bfloat16), support_mid, False
    )
    fine_coef = 0.5 * own_data + scale_e1 * lax.psum_scatter(
        fine_part, "col", scatter_dimension=0, tiled=True
    )
    fine_total = lax.psum(fine_square / col_count, ("row", "col"))
    fine_norm = fine_total / (rows_fine * row_count * fields)
    return (fine_coef, mid_coef, coarse_coef, jnp.stack([fine_norm]))


def solution(mesh):
    return jax.shard_map(
        per_device,
        mesh=mesh,
        in_specs=(
            P("row", None),
            P(None, "row"),
            P(None, "row"),
            P(None, "row"),
            P("row", "col", None, None),
            P("row", "col", None, None),
            P("row", "col", None, None),
            P("row", "col"),
        ),
        out_specs=(P(("row", "col"), None), P("col", None), P("row", None), P()),
        check_vma=False,
    )
```

profile of v0, /device:TPU:0, one launch (start us, length us, event | category | flops | bytes accessed | tf_op | source)
XLA Modules:
  0.0 501.4 jit_solution(3732552858694689181)
XLA Ops:
  7.3 1.7 dynamic-slice_select_fusion
  11.9 8.5 %all-reduce = (bf16[2,256]{1,0:T(2,128)(2,1)S(1)}, bf16[2,8,128]{2,0,1:T(2,128)(2,1)S(1)}) all-reduce(bf16[2,256]{1,0:T(2,128)(2,1)S(1)} %broadcast_select_fusion.1, bf16[2,8,128]{2,0,1:T(2,128)(2,1)S(1)} %fusion.64), channel_id=1, replica_groups=mesh['row'=4,'col'=8] {'row'}, use_global_device_ids=true, to_apply=%region_0.1 | all-reduce | flops 2560 | bytes 10240 | tf_op jit(solution)/shard_map/psum | solution.py:15
  20.4 24.9 %all-reduce.8.cloned.1.call-done = bf16[8,128,128]{2,1,0:T(8,128)(2,1)} async-done(((bf16[8,128,128]{2,1,0:T(8,128)(2,1)}), bf16[8,128,128]{2,1,0:T(8,128)(2,1)}) %all-reduce.8.cloned.1.call-update) | async-done | bytes 262160 | tf_op jit(solution)/shard_map/psum | solution.py:15
  46.3 15.2 %while.40 = (s32[]{:T(128)}, f32[16,128,128]{2,1,0:T(8,128)S(1)}, s32[3,16]{1,0:T(4,128)S(1)}, bf16[2,16,128]{2,0,1:T(2,128)(2,1)S(1)}, s32[3,16]{1,0:T(4,128)S(...) while((s32[]{:T(128)}, f32[16,128,128]{2,1,0:T(8,128)S(1)}, ...), condition=%wide.region_5.6_spmd, body=%wide.region_3.5_spmd.sunk | while | flops 71051360 | bytes 5956313 | solution.py:53
  48.2 1.5 fusion.118
  49.7 1.6 scatter_fusion
  54.8 1.6 scatter_fusion
  59.9 1.6 scatter_fusion
  63.9 77.0 %all-reduce.10.cloned.1.call-done = f32[2048,128]{1,0:T(8,128)} async-done(((f32[2048,128]{1,0:T(8,128)}), f32[2048,128]{1,0:T(8,128)}) %all-reduce.10.cloned.1.call-update) | async-done | bytes 1048592 | tf_op jit(solution)/shard_map/psum | solution.py:84
  140.9 2.2 multiply_reduce_fusion
  143.1 14.7 %while.41 = (s32[]{:T(128)}, f32[2,128,128]{2,1,0:T(8,128)S(1)}, s32[5,4]{1,0:T(8,128)S(1)}, s32[5,4]{1,0:T(8,128)S(1)}, bf16[2,16,128]{2,0,1:T(2,128)(2,1)S(1)}...) while((s32[]{:T(128)}, f32[2,128,128]{2,1,0:T(8,128)S(1)}, ...), condition=%wide.region_9.10_spmd, body=%wide.region_7.9_spmd.sunk | while | flops 17764376 | bytes 1495289 | solution.py:53
  158.6 31.5 %all-reduce.12.cloned.1.call-done = f32[256,128]{1,0:T(8,128)} async-done(((f32[256,128]{1,0:T(8,128)}), f32[256,128]{1,0:T(8,128)}) %all-reduce.12.cloned.1.call-update) | async-done | bytes 131088 | tf_op jit(solution)/shard_map/psum | solution.py:90
  193.5 71.1 %all-reduce.14.cloned.1.call-done = f32[512,128]{1,0:T(8,128)} async-done(((f32[512,128]{1,0:T(8,128)}), f32[512,128]{1,0:T(8,128)}) %all-reduce.14.cloned.1.call-update) | async-done | bytes 262160 | tf_op jit(solution)/shard_map/psum | solution.py:95
  264.6 1.6 fusion.57
  266.2 31.9 %all-reduce.16.cloned.1.call-done = bf16[256,128]{1,0:T(8,128)(2,1)} async-done(((bf16[256,128]{1,0:T(8,128)(2,1)}), bf16[256,128]{1,0:T(8,128)(2,1)}) %all-reduce.16.cloned.1.call-update) | async-done | bytes 65552 | tf_op jit(solution)/shard_map/psum | solution.py:15
  299.2 37.1 %psum.91 = f32[64,128]{1,0:T(8,128)S(1)} all-reduce(f32[64,128]{1,0:T(8,128)S(1)} %fusion.56), channel_id=1, replica_groups=mesh['row'=4,'col'=8] {'col'}, use_global_device_ids=true, to_apply=%region_14.15 | all-reduce | flops 8192 | bytes 65536 | tf_op jit(solution)/shard_map/psum | solution.py:103
  336.5 10.8 %psum.92 = bf16[32,128]{0,1:T(8,128)(2,1)S(1)} all-reduce(f32[32,128]{0,1:T(8,128)S(1)} %convolution_bitcast_fusion), channel_id=1, replica_groups=mesh['row'=4,'col'=8] {'row'}, use_global_device_ids=true, to_apply=%region_15.16 | all-reduce | flops 4096 | bytes 24576 | tf_op jit(solution)/shard_map/psum | solution.py:108
  347.5 33.0 %psum.93 = f32[64,128]{1,0:T(8,128)S(1)} all-reduce(f32[64,128]{1,0:T(8,128)S(1)} %convolution_bitcast_fusion.1), channel_id=1, replica_groups=mesh['row'=4,'col'=8] {'col'}, use_global_device_ids=true, to_apply=%region_16.17 | all-reduce | flops 8192 | bytes 65536 | tf_op jit(solution)/shard_map/psum | solution.py:110
  381.6 28.0 %all-reduce.18.cloned.1.call-done = f32[256,128]{1,0:T(8,128)} async-done(((f32[256,128]{1,0:T(8,128)}), f32[256,128]{1,0:T(8,128)}) %all-reduce.18.cloned.1.call-update) | async-done | bytes 131088 | tf_op jit(solution)/shard_map/psum | solution.py:117
  409.5 1.6 fusion.82
  411.2 14.8 %while.42 = (s32[]{:T(128)}, f32[16,128,128]{2,1,0:T(8,128)S(1)}, s32[5,4]{1,0:T(8,128)S(1)}, bf16[2,16,128]{2,0,1:T(2,128)(2,1)S(1)}, s32[5,4]{1,0:T(8,128)S(1)...) while((s32[]{:T(128)}, f32[16,128,128]{2,1,0:T(8,128)S(1)}, ...), condition=%wide.region_20.21_spmd, body=%wide.region_18.20_spmd.sunk | while | flops 17764376 | bytes 1495289 | solution.py:53
  427.7 39.5 %psum.95 = f32[]{:T(128)} all-reduce(f32[]{:T(128)S(6)} %div.39), channel_id=1, replica_groups=mesh['row'=4,'col'=8] {'row','col'}, use_global_device_ids=true, to_apply=%region_23.24 | all-reduce | flops 1 | bytes 8 | tf_op jit(solution)/shard_map/psum | solution.py:124
  467.8 24.0 %reduce-scatter.2.cloned.1.call-done = f32[256,128]{1,0:T(8,128)} async-done(((f32[2048,128]{1,0:T(8,128)}), f32[256,128]{1,0:T(8,128)}) %reduce-scatter.2.cloned.1.call-update) | async-done | bytes 131088 | tf_op jit(solution)/shard_map/reduce_scatter | solution.py:121
  491.8 1.6 multiply_add_fusion
  (228 shorter events, 51.4 us)
Async XLA Ops:
  7.2 329.1 %copy-start = (bf16[64,32]{0,1:T(8,128)(2,1)S(1)}, bf16[64,32]{0,1:T(8,128)(2,1)}, u32[]{:S(2)}) copy-start(bf16[64,32]{0,1:T(8,128)(2,1)} %param.21) | copy-start | bytes 12292
  7.2 38.2 %all-reduce.8.cloned.1.call-start = ((), (), s32[]{:S(2)}) async-start(), calls=%async_computation.1 | async-start | bytes 524288 | tf_op jit(solution)/shard_map/psum | solution.py:15
  9.0 131.9 %all-reduce.10.cloned.1.call-start = ((), (), s32[]{:S(2)}) async-start(), calls=%async_computation.2 | async-start | bytes 2097152 | tf_op jit(solution)/shard_map/psum | solution.py:84
  9.0 0.7 copy-start.11
  9.7 0.7 copy-start.12
  10.4 0.7 copy-start.10
  11.2 0.7 copy-start.8
  45.4 0.9 copy-start.2
  61.5 1.0 copy-start.1
  61.5 1.1 copy-start.13
  61.6 79.4 %copy-start.6 = (bf16[2048,128]{1,0:T(8,128)(2,1)S(1)}, bf16[2048,128]{1,0:T(8,128)(2,1)}, u32[]{:S(2)}) copy-start(bf16[2048,128]{1,0:T(8,128)(2,1)} %param.14) | copy-start | bytes 1572868
  62.6 127.5 %all-reduce.12.cloned.1.call-start = ((), (), s32[]{:S(2)}) async-start(), calls=%async_computation.3 | async-start | bytes 262144 | tf_op jit(solution)/shard_map/psum | solution.py:90
  157.9 0.7 copy-start.3
  158.5 106.1 %all-reduce.14.cloned.1.call-start = ((), (), s32[]{:S(2)}) async-start(), calls=%async_computation.4 | async-start | bytes 524288 | tf_op jit(solution)/shard_map/psum | solution.py:95
  192.7 0.7 copy-start.5
  192.7 0.8 copy-start.14
  193.4 104.7 %all-reduce.16.cloned.1.call-start = ((), (), s32[]{:S(2)}) async-start(), calls=%async_computation.5 | async-start | bytes 131072 | tf_op jit(solution)/shard_map/psum | solution.py:15
  193.5 104.6 %copy-start.7 = (f32[256,128]{1,0:T(8,128)S(1)}, f32[256,128]{1,0:T(8,128)}, u32[]{:S(2)}) copy-start(f32[256,128]{1,0:T(8,128)} %all-reduce.12.cloned.1.call-done) | copy-start | bytes 393220
  266.2 143.4 %all-reduce.18.cloned.1.call-start = ((), (), s32[]{:S(2)}) async-start(), calls=%async_computation.6 | async-start | bytes 262144 | tf_op jit(solution)/shard_map/psum | solution.py:117
  380.5 1.0 copy-start.9
  381.5 110.3 %reduce-scatter.2.cloned.1.call-start = ((), (), s32[]{:S(2)}) async-start(), calls=%async_computation.7 | async-start | bytes 1179648 | tf_op jit(solution)/shard_map/reduce_scatter | solution.py:121
  426.0 1.0 copy-start.4
Sparse Core Ops, SparseCore 0:
  10.3 34.9 all-reduce.7
  62.7 78.1 all-reduce.9
  158.7 31.3 all-reduce.11
  193.6 70.9 all-reduce.13
  267.3 30.7 all-reduce.15
  381.6 27.8 all-reduce.17
  427.2 64.5 reduce-scatter.1
where the time goes:
time: 502 us; the launch traced here: 501 us
  waiting for transfers between devices  288 us (57%)
  blocking collectives  129 us (26%)
  local copies, waits for them, and re-layouts  31.9 us (6%)
  other arithmetic  23.1 us (5%)
  between operations  16.8 us (3%)
  matrix products  10.9 us (2%)
    psum x1, waiting for transfers between devices, per_device(): product_whole = lax.psum(product_part, 'col')  77 us
    psum x1, waiting for transfers between devices, per_device(): mid_whole = (scale_a1 * lax.psum(mid_part, 'col')).astype(jnp.bfloat16)  71.1 us
    psum x2, waiting for transfers between devices, spread(): return lax.psum(jnp.where(mine, x, jnp.zeros_like(x)), axis)  56.8 us
    psum x1, blocking collectives, per_device(): fine_total = lax.psum(fine_square / col_count, ('row', 'col'))  39.5 us
    psum x1, blocking collectives, per_device(): coarse_sum = lax.psum(coarse_part, 'col')  37.1 us
    psum x1, blocking collectives, per_device(): coarse_coef = lax.psum(coarse_part_two, 'col')  33 us
    psum x1, waiting for transfers between devices, per_device(): restrict_sum = lax.psum(restrict_part, 'row')  31.5 us
    psum x1, waiting for transfers between devices, per_device(): mid_coef = 0.5 * mid_data + scale_e2 * lax.psum(prolong_part, 'row')  28 us
  transfers between devices with their start and end apart: 7, of which 7 were waited for; matrix products, arithmetic and copies ran while one was open for 0% of the time, Pallas kernels for 0%

commit v1 on v0

--- a/solution.py
+++ b/solution.py
@@ -8,6 +8,16 @@
 support_fine = 0.35
 support_mid = 0.55
 support_coarse = 0.8
+
+
+def strips_all_make(s0):
+    field_out = s0
+    p_count = lax.axis_size("col")
+    for hop_no in [it for it in (1, 2, 4, 8, 16) if it < p_count]:
+        field_out = field_out + lax.ppermute(
+            field_out, "col", [(p, p ^ hop_no) for p in range(p_count)]
+        )
+    return field_out
 
 
 def spread(x, axis, root):
@@ -107,7 +117,7 @@
     )
     halfway = lax.psum(halfway_part, "row").astype(jnp.bfloat16)
     coarse_part_two = jnp.dot(factor, halfway, preferred_element_type=jnp.float32)
-    coarse_coef = lax.psum(coarse_part_two, "col")
+    coarse_coef = strips_all_make(coarse_part_two)
     prolong_part = lax.dot_general(
         coarse_kernel,
         coarse_coef.astype(jnp.bfloat16),

time: 502 us -> 481 us (0.958)
  blocking collectives: 129 us -> 96 us
  waiting for transfers between devices: 288 us -> 301 us
    psum x1 -> x0, blocking collectives: 33 us -> none  [per_device(): coarse_coef = lax.psum(coarse_part_two, 'col')]
    ppermute x0 -> x3, waiting for transfers between devices: none -> 12.6 us  [strips_all_make(): lax.ppermute(field_out, 'col', [(p, p ^ hop_no) for p in range(p_count)])]
  transfers between devices with their start and end apart: 7 -> 10, of which waited for: 7 -> 10; matrix products, arithmetic and copies ran while one was open for 0% -> 0% of each run, Pallas kernels for 0% -> 0%
where the time goes in v1:
time: 481 us
  waiting for transfers between devices  301 us (63%)
  blocking collectives  96 us (20%)
  local copies, waits for them, and re-layouts  31.8 us (7%)
  other arithmetic  23.1 us (5%)
  between operations  16.8 us (3%)
  matrix products  11 us (2%)
    psum x1, waiting for transfers between devices, per_device(): product_whole = lax.psum(product_part, 'col')  77.1 us
    psum x1, waiting for transfers between devices, per_device(): mid_whole = (scale_a1 * lax.psum(mid_part, 'col')).astype(jnp.bfloat16)  71.1 us
    psum x2, waiting for transfers between devices, spread(): return lax.psum(jnp.where(mine, x, jnp.zeros_like(x)), axis)  56.8 us
    psum x1, blocking collectives, per_device(): fine_total = lax.psum(fine_square / col_count, ('row', 'col'))  39.5 us
    psum x1, blocking collectives, per_device(): coarse_sum = lax.psum(coarse_part, 'col')  37.1 us
    psum x1, waiting for transfers between devices, per_device(): restrict_sum = lax.psum(restrict_part, 'row')  31.5 us
    psum x1, waiting for transfers between devices, per_device(): mid_coef = 0.5 * mid_data + scale_e2 * lax.psum(prolong_part, 'row')  28 us
    reduce_scatter x1, waiting for transfers between devices, per_device(): lax.psum_scatter(fine_part, 'col', scatter_dimension=0, tiled=True)  23.7 us
  transfers between devices with their start and end apart: 10, of which 10 were waited for; matrix products, arithmetic and copies ran while one was open for 0% of the time, Pallas kernels for 0%

profile of v1, /device:TPU:0, one launch (start us, length us, event | category | flops | bytes accessed | tf_op | source)
XLA Modules:
  0.0 480.7 jit_solution(11339235179764697048)
XLA Ops:
  7.3 1.7 dynamic-slice_select_fusion
  11.9 8.5 %all-reduce = (bf16[2,256]{1,0:T(2,128)(2,1)S(1)}, bf16[2,8,128]{2,0,1:T(2,128)(2,1)S(1)}) all-reduce(bf16[2,256]{1,0:T(2,128)(2,1)S(1)} %broadcast_select_fusion.1, bf16[2,8,128]{2,0,1:T(2,128)(2,1)S(1)} %fusion.64), channel_id=1, replica_groups=mesh['row'=4,'col'=8] {'row'}, use_global_device_ids=true, to_apply=%region_0.1 | all-reduce | flops 2560 | bytes 10240 | tf_op jit(solution)/shard_map/psum | solution.py:25
  20.4 24.9 %all-reduce.8.cloned.1.call-done = bf16[8,128,128]{2,1,0:T(8,128)(2,1)} async-done(((bf16[8,128,128]{2,1,0:T(8,128)(2,1)}), bf16[8,128,128]{2,1,0:T(8,128)(2,1)}) %all-reduce.8.cloned.1.call-update) | async-done | bytes 262160 | tf_op jit(solution)/shard_map/psum | solution.py:25
  46.3 15.2 %while.40 = (s32[]{:T(128)}, f32[16,128,128]{2,1,0:T(8,128)S(1)}, s32[3,16]{1,0:T(4,128)S(1)}, bf16[2,16,128]{2,0,1:T(2,128)(2,1)S(1)}, s32[3,16]{1,0:T(4,128)S(...) while((s32[]{:T(128)}, f32[16,128,128]{2,1,0:T(8,128)S(1)}, ...), condition=%wide.region_5.6_spmd, body=%wide.region_3.5_spmd.sunk | while | flops 71051360 | bytes 5956313 | solution.py:63
  49.7 1.6 scatter_fusion
  54.8 1.6 scatter_fusion
  59.9 1.6 scatter_fusion
  63.9 77.1 %all-reduce.10.cloned.1.call-done = f32[2048,128]{1,0:T(8,128)} async-done(((f32[2048,128]{1,0:T(8,128)}), f32[2048,128]{1,0:T(8,128)}) %all-reduce.10.cloned.1.call-update) | async-done | bytes 1048592 | tf_op jit(solution)/shard_map/psum | solution.py:94
  140.9 2.1 multiply_reduce_fusion
  143.1 14.7 %while.41 = (s32[]{:T(128)}, f32[2,128,128]{2,1,0:T(8,128)S(1)}, s32[5,4]{1,0:T(8,128)S(1)}, s32[5,4]{1,0:T(8,128)S(1)}, bf16[2,16,128]{2,0,1:T(2,128)(2,1)S(1)}...) while((s32[]{:T(128)}, f32[2,128,128]{2,1,0:T(8,128)S(1)}, ...), condition=%wide.region_9.10_spmd, body=%wide.region_7.9_spmd.sunk | while | flops 17764376 | bytes 1495289 | solution.py:63
  158.6 31.5 %all-reduce.12.cloned.1.call-done = f32[256,128]{1,0:T(8,128)} async-done(((f32[256,128]{1,0:T(8,128)}), f32[256,128]{1,0:T(8,128)}) %all-reduce.12.cloned.1.call-update) | async-done | bytes 131088 | tf_op jit(solution)/shard_map/psum | solution.py:100
  193.5 71.1 %all-reduce.14.cloned.1.call-done = f32[512,128]{1,0:T(8,128)} async-done(((f32[512,128]{1,0:T(8,128)}), f32[512,128]{1,0:T(8,128)}) %all-reduce.14.cloned.1.call-update) | async-done | bytes 262160 | tf_op jit(solution)/shard_map/psum | solution.py:105
  266.2 31.9 %all-reduce.16.cloned.1.call-done = bf16[256,128]{1,0:T(8,128)(2,1)} async-done(((bf16[256,128]{1,0:T(8,128)(2,1)}), bf16[256,128]{1,0:T(8,128)(2,1)}) %all-reduce.16.cloned.1.call-update) | async-done | bytes 65552 | tf_op jit(solution)/shard_map/psum | solution.py:25
  299.2 37.1 %psum.84 = f32[64,128]{1,0:T(8,128)S(1)} all-reduce(f32[64,128]{1,0:T(8,128)S(1)} %fusion.56), channel_id=1, replica_groups=mesh['row'=4,'col'=8] {'col'}, use_global_device_ids=true, to_apply=%region_14.15 | all-reduce | flops 8192 | bytes 65536 | tf_op jit(solution)/shard_map/psum | solution.py:113
  336.4 10.8 %psum.85 = bf16[32,128]{0,1:T(8,128)(2,1)S(1)} all-reduce(f32[32,128]{0,1:T(8,128)S(1)} %convolution_bitcast_fusion), channel_id=1, replica_groups=mesh['row'=4,'col'=8] {'row'}, use_global_device_ids=true, to_apply=%region_15.16 | all-reduce | flops 4096 | bytes 24576 | tf_op jit(solution)/shard_map/psum | solution.py:118
  347.5 3.9 collective-permute-done
  351.4 3.9 collective-permute-done.1
  355.3 4.8 collective-permute-done.2
  361.2 28.0 %all-reduce.18.cloned.1.call-done = f32[256,128]{1,0:T(8,128)} async-done(((f32[256,128]{1,0:T(8,128)}), f32[256,128]{1,0:T(8,128)}) %all-reduce.18.cloned.1.call-update) | async-done | bytes 131088 | tf_op jit(solution)/shard_map/psum | solution.py:127
  389.2 1.6 fusion.82
  390.9 14.8 %while.42 = (s32[]{:T(128)}, f32[16,128,128]{2,1,0:T(8,128)S(1)}, s32[5,4]{1,0:T(8,128)S(1)}, bf16[2,16,128]{2,0,1:T(2,128)(2,1)S(1)}, s32[5,4]{1,0:T(8,128)S(1)...) while((s32[]{:T(128)}, f32[16,128,128]{2,1,0:T(8,128)S(1)}, ...), condition=%wide.region_19.20_spmd, body=%wide.region_17.19_spmd.sunk | while | flops 17764376 | bytes 1495289 | solution.py:63
  407.3 39.5 %psum.87 = f32[]{:T(128)} all-reduce(f32[]{:T(128)S(6)} %div.39), channel_id=1, replica_groups=mesh['row'=4,'col'=8] {'row','col'}, use_global_device_ids=true, to_apply=%region_22.23 | all-reduce | flops 1 | bytes 8 | tf_op jit(solution)/shard_map/psum | solution.py:134
  447.4 23.7 %reduce-scatter.2.cloned.1.call-done = f32[256,128]{1,0:T(8,128)} async-done(((f32[2048,128]{1,0:T(8,128)}), f32[256,128]{1,0:T(8,128)}) %reduce-scatter.2.cloned.1.call-update) | async-done | bytes 131088 | tf_op jit(solution)/shard_map/reduce_scatter | solution.py:131
  471.1 1.6 multiply_add_fusion
  (236 shorter events, 54.4 us)
Async XLA Ops:
  7.2 329.1 %copy-start = (bf16[64,32]{0,1:T(8,128)(2,1)S(1)}, bf16[64,32]{0,1:T(8,128)(2,1)}, u32[]{:S(2)}) copy-start(bf16[64,32]{0,1:T(8,128)(2,1)} %param.21) | copy-start | bytes 12292
  7.2 38.2 %all-reduce.8.cloned.1.call-start = ((), (), s32[]{:S(2)}) async-start(), calls=%async_computation.1 | async-start | bytes 524288 | tf_op jit(solution)/shard_map/psum | solution.py:25
  9.0 131.9 %all-reduce.10.cloned.1.call-start = ((), (), s32[]{:S(2)}) async-start(), calls=%async_computation.2 | async-start | bytes 2097152 | tf_op jit(solution)/shard_map/psum | solution.py:94
  9.0 0.7 copy-start.11
  9.7 0.7 copy-start.12
  10.4 0.7 copy-start.10
  11.2 0.7 copy-start.8
  45.4 0.9 copy-start.2
  61.5 1.0 copy-start.1
  61.5 1.1 copy-start.13
  61.6 79.4 %copy-start.6 = (bf16[2048,128]{1,0:T(8,128)(2,1)S(1)}, bf16[2048,128]{1,0:T(8,128)(2,1)}, u32[]{:S(2)}) copy-start(bf16[2048,128]{1,0:T(8,128)(2,1)} %param.14) | copy-start | bytes 1572868
  62.6 127.5 %all-reduce.12.cloned.1.call-start = ((), (), s32[]{:S(2)}) async-start(), calls=%async_computation.3 | async-start | bytes 262144 | tf_op jit(solution)/shard_map/psum | solution.py:100
  158.5 106.1 %all-reduce.14.cloned.1.call-start = ((), (), s32[]{:S(2)}) async-start(), calls=%async_computation.4 | async-start | bytes 524288 | tf_op jit(solution)/shard_map/psum | solution.py:105
  192.7 0.7 copy-start.5
  192.7 0.8 copy-start.14
  193.4 104.7 %all-reduce.16.cloned.1.call-start = ((), (), s32[]{:S(2)}) async-start(), calls=%async_computation.5 | async-start | bytes 131072 | tf_op jit(solution)/shard_map/psum | solution.py:25
  193.5 104.6 %copy-start.7 = (f32[256,128]{1,0:T(8,128)S(1)}, f32[256,128]{1,0:T(8,128)}, u32[]{:S(2)}) copy-start(f32[256,128]{1,0:T(8,128)} %all-reduce.12.cloned.1.call-done) | copy-start | bytes 393220
  266.2 123.0 %all-reduce.18.cloned.1.call-start = ((), (), s32[]{:S(2)}) async-start(), calls=%async_computation.6 | async-start | bytes 262144 | tf_op jit(solution)/shard_map/psum | solution.py:127
  347.5 3.9 collective-permute-start
  351.4 3.9 collective-permute-start.1
  355.3 4.8 %collective-permute-start.2 = (f32[64,128]{1,0:T(8,128)S(1)}, f32[64,128]{1,0:T(8,128)S(1)}, u32[]{:S(2)}, u32[]{:S(2)}) collective-permute-start(f32[64,128]{1,0:T(8,128)S(1)} %add.252), channel_id=1, source_target_pairs={{0,4},{1,5},{2,6},{3,7},{4,0},{5,1},{6,2},{7,3},{8,12},{9,13},{10,... | collective-permute-start | bytes 98312 | tf_op jit(solution)/shard_map/ppermute | solution.py:17
  360.2 1.0 copy-start.9
  361.1 109.9 %reduce-scatter.2.cloned.1.call-start = ((), (), s32[]{:S(2)}) async-start(), calls=%async_computation.7 | async-start | bytes 1179648 | tf_op jit(solution)/shard_map/reduce_scatter | solution.py:131
  405.6 1.0 copy-start.4
  (1 other events, 0.7 us)
Sparse Core Ops, SparseCore 0:
  10.3 34.9 all-reduce.7
  62.7 78.1 all-reduce.9
  158.6 31.3 all-reduce.11
  193.5 71.0 all-reduce.13
  267.3 30.7 all-reduce.15
  361.3 27.8 all-reduce.17
  406.8 64.2 reduce-scatter.1
